TPU v7x, 32 devices: a whole 2x2x4 slice. The times are simulated.
32 devices in a mesh: groups: 2 (over y), ep: 16 (over z, x, core).
Axes of the slice: x: 2, y: 2, z: 4, core: 2. Of those that a mesh axis runs over, the one named last changes fastest.
Arguments:
- tokens: bfloat16 [4096, 1440], P(('groups', 'ep')), parts along dimension 0, may hold values from -6 to 6
- expert_ids: int32 [4096, 4], P(('groups', 'ep')), parts along dimension 0, may hold values from 0 to 15, as said below
- combine: float32 [4096, 4], P(('groups', 'ep')), parts along dimension 0, may hold values from 0.05 to 1
- gate_weight: bfloat16 [16, 1440, 1440], P('ep'), may hold values from -0.15625 to 0.15625
- up_weight: bfloat16 [16, 1440, 1440], P('ep'), may hold values from -0.15625 to 0.15625
- down_weight: bfloat16 [16, 1440, 1440], P('ep'), may hold values from -0.15625 to 0.15625
Outputs:
- mixture: bfloat16 [4096, 1440], P(('groups', 'ep')), parts along dimension 0
There are 2 independent parts, one for each index of `groups`. A program takes and returns all parts, laid end to end along the dimension named above; an argument that names none is the same for every part. Nothing has to cross between parts.
Inputs may be any that keep to these rules, and one draw needn't show every extreme that they name: `expert_ids`: each row names 4 different experts. In the rows of one device (aligned blocks of 128 rows) no expert is named more than 64 times, and some expert is named exactly 64 times in every block.
All inputs are finite; a program needn't handle non-finite values.
Results may differ from a plain program's by a relative error of at most 0.0058.
Values may be sent and summed in bfloat16 or wider, within the bound.
A program may use at most 64 MiB of HBM per device.

v0:
```python
import functools

import jax
import jax.numpy as jnp
from jax import lax
from jax.experimental import pallas as pl
from jax.experimental.pallas import tpu as pltpu
from jax.sharding import PartitionSpec as P

MESH = pl.DeviceIdType.MESH

alpha_gate = 1.702


def run_expert_block(row_block, gate_proj, up_proj, down_proj):
    gate_part = jnp.dot(row_block, gate_proj, preferred_element_type=jnp.float32)
    up_part = jnp.dot(row_block, up_proj, preferred_element_type=jnp.float32)
    hidden = ((up_part + 1.0) * gate_part * jax.nn.sigmoid(alpha_gate * gate_part)).astype(
        jnp.bfloat16
    )
    return jnp.dot(hidden, down_proj, preferred_element_type=jnp.float32).astype(jnp.bfloat16)


def line_kernel(
    tok_hbm, mix_ref, gate_hbm, up_hbm, down_hbm, out_ref,
    x_buf, w_in, gate_w, up_w, down_w, rows, part, other, quad, rx, ru, rd,
    load_sem, agz_s, agx_s, agp_s, w_s, pc_s, rsx_s, rsz_s,
    x_r, xp_r, w_r, q_r, rx_r, ru_r, rd_r,
    *, members, capacity, pieces,
):
    length = members // 4
    here = tok_hbm.shape[0]
    me = lax.axis_index("ep")
    z, x, c = me // 4, (me // 2) % 2, me % 2
    pc = 1 - c

    def member(zz, xx, cc):
        return (zz * 2 + xx) * 2 + cc

    across = member(z, 1 - x, c)
    partner = member(z, x, pc)
    above = member(jnp.minimum(z + 1, length - 1), x, c)
    below = member(jnp.maximum(z - 1, 0), x, c)

    def send(src, dst, ssem, rsem, to):
        return pltpu.make_async_remote_copy(
            src_ref=src, dst_ref=dst, send_sem=ssem, recv_sem=rsem,
            device_id={"ep": to}, device_id_type=MESH,
        )

    loads = [
        pltpu.make_async_copy(tok_hbm, x_buf.at[z, x, c], load_sem.at[0]),
        pltpu.make_async_copy(gate_hbm, gate_w, load_sem.at[1]),
        pltpu.make_async_copy(up_hbm, up_w, load_sem.at[2]),
        pltpu.make_async_copy(down_hbm, down_w, load_sem.at[3]),
    ]
    for load in loads:
        load.start()

    barrier = pltpu.get_barrier_semaphore()
    for step in range(1, members):
        to = lax.rem(me + step, members)
        pl.semaphore_signal(barrier, inc=1, device_id={"ep": to}, device_id_type=MESH)
    pl.semaphore_wait(barrier, members - 1)

    def weights_copy(step):
        to = lax.rem(me + step, members)
        return send(mix_ref.at[to], w_in.at[me], w_s.at[step], w_r.at[me], to)

    def weights_arrival(step):
        origin = lax.rem(me + step, members)
        return send(mix_ref.at[origin], w_in.at[origin], w_s.at[step], w_r.at[origin], origin)

    size = here // pieces

    def cut(piece):
        return pl.ds(pl.multiple_of(piece * size, size), size)

    def ag(zz, piece, ssem, to):
        slot = x_buf.at[zz, x, c, cut(piece)]
        return send(slot, slot, ssem, x_r.at[zz, x, piece], to)

    def to_above(zz, piece):
        return ag(zz, piece, agz_s.at[zz, 0, piece], above)

    def to_below(zz, piece):
        return ag(zz, piece, agz_s.at[zz, 1, piece], below)

    def to_across(zz, piece):
        return ag(zz, piece, agx_s.at[zz, piece], across)

    def to_partner(zz, xx):
        slot = x_buf.at[zz, xx, c]
        return send(slot, slot, agp_s.at[zz, xx], xp_r.at[zz, xx], partner)

    def goes_up(zz):
        return jnp.logical_and(zz <= z, z < length - 1)

    def goes_down(zz):
        return jnp.logical_and(zz >= z, z > 0)

    def each_piece(act):
        def one(piece, carry):
            act(piece)
            return carry

        lax.fori_loop(0, pieces, one, 0)

    def forward(zz, arriving):
        def one(piece):
            if arriving:
                arrival(zz, x, piece)

            @pl.when(goes_up(zz))
            def _():
                to_above(zz, piece).start()

            @pl.when(goes_down(zz))
            def _():
                to_below(zz, piece).start()

            to_across(zz, piece).start()

        each_piece(one)
        to_partner(zz, x).start()

    def arrival(zz, xx, piece):
        slot = x_buf.at[zz, xx, c, cut(piece)]
        send(slot, slot, agx_s.at[zz, piece], x_r.at[zz, xx, piece], partner).wait_recv()

    def partner_arrival(zz, xx):
        slot = x_buf.at[zz, xx, pc]
        send(slot, slot, agp_s.at[zz, xx], xp_r.at[zz, xx], partner).wait_recv()

    near = jnp.minimum(z, length - 1 - z)

    def nearest(k):
        along = near + jnp.where(k % 2 == 1, (k + 1) // 2, -(k // 2))
        low = jnp.where(k <= 2 * near, along, k)
        return jnp.where(z == near, low, length - 1 - low)

    loads[0].wait()
    forward(z, False)
    for step in range(1, members):
        weights_copy(step).start()
    w_in[me] = mix_ref[me]
    for step in range(1, members):
        weights_arrival(step).wait_recv()

    row_at = lax.broadcasted_iota(jnp.int32, (capacity, here), 0).astype(jnp.float32)
    before = (
        lax.broadcasted_iota(jnp.int32, (here, here), 0)
        < lax.broadcasted_iota(jnp.int32, (here, here), 1)
    ).astype(jnp.bfloat16)

    def picker(zz, xx, cc):
        weight = w_in[member(zz, xx, cc)]
        named = weight > 0.0
        flags = jnp.broadcast_to(named.astype(jnp.float32), (8, here)).astype(jnp.bfloat16)
        rank = jnp.dot(flags, before, preferred_element_type=jnp.float32)[0:1, :]
        pick = jnp.where(named, rank, -1.0) == row_at
        scale = jnp.sum(jnp.where(pick, weight, 0.0), axis=1, keepdims=True)
        return pick.astype(jnp.float32).astype(jnp.bfloat16), scale

    def compute(zz, xx):
        picks, scales = [], []
        for side, cc in enumerate((c, pc)):
            pick, scale = picker(zz, xx, cc)
            picks.append(pick)
            scales.append(scale)
            rows[side * capacity : (side + 1) * capacity, :] = jnp.dot(
                pick, x_buf[zz, xx, cc], preferred_element_type=jnp.float32
            ).astype(jnp.bfloat16)
        block = rows[...]
        gate = jnp.dot(block, gate_w[...], preferred_element_type=jnp.float32)
        up = jnp.dot(block, up_w[...], preferred_element_type=jnp.float32)
        hidden = ((up + 1.0) * gate * jax.nn.sigmoid(alpha_gate * gate)).astype(jnp.bfloat16)
        answer = jnp.dot(hidden, down_w[...], preferred_element_type=jnp.float32)
        for side, dst in enumerate((part, other)):
            scaled = (
                answer[side * capacity : (side + 1) * capacity, :]
                .astype(jnp.bfloat16).astype(jnp.float32) * scales[side]
            ).astype(jnp.bfloat16)
            dst[zz, xx] = lax.dot_general(
                picks[side], scaled, (((0,), (0,)), ((), ())),
                preferred_element_type=jnp.float32,
            ).astype(jnp.bfloat16)

    def answer_copy(zz, xx):
        return send(other.at[zz, xx], quad.at[zz, xx], pc_s.at[zz, xx], q_r.at[zz, xx], partner)

    def across_copy(zz, piece):
        return send(
            part.at[zz, 1 - x, cut(piece)], rx.at[zz, cut(piece)],
            rsx_s.at[zz, piece], rx_r.at[zz, piece], across,
        )

    def all_across(zz):
        each_piece(lambda piece: across_copy(zz, piece).start())

    def join_partner(zz, xx):
        answer_copy(zz, xx).wait_recv()
        part[zz, xx] = (
            part[zz, xx].astype(jnp.float32) + quad[zz, xx].astype(jnp.float32)
        ).astype(jnp.bfloat16)

    def up_copy(zz, xx, piece):
        return send(
            part.at[zz, xx, cut(piece)], ru.at[zz, xx, cut(piece)],
            rsz_s.at[zz, xx, piece], ru_r.at[zz, xx, piece], above,
        )

    def down_copy(zz, xx, piece):
        return send(
            part.at[zz, xx, cut(piece)], rd.at[zz, xx, cut(piece)],
            rsz_s.at[zz, xx, piece], rd_r.at[zz, xx, piece], below,
        )

    def add_in(zz, xx, piece, addend):
        part[zz, xx, cut(piece)] = (
            part[zz, xx, cut(piece)].astype(jnp.float32) + addend.astype(jnp.float32)
        ).astype(jnp.bfloat16)

    def take_across(zz, piece):
        across_copy(zz, piece).wait_recv()
        add_in(zz, x, piece, rx[zz, cut(piece)])

    def column(j):
        return jnp.where(c == 1, x, (x + 1 + j) % 2)

    def chain(zz):
        def one(step, carry):
            xx, piece = column(step // pieces), step % pieces

            @pl.when(c == 1)
            def _():
                take_across(zz, piece)

            @pl.when(jnp.logical_and(zz >= z, z > 0))
            def _():
                up_copy(zz, xx, piece).wait_recv()
                add_in(zz, xx, piece, ru[zz, xx, cut(piece)])

            @pl.when(jnp.logical_and(zz <= z, z < length - 1))
            def _():
                down_copy(zz, xx, piece).wait_recv()
                add_in(zz, xx, piece, rd[zz, xx, cut(piece)])

            @pl.when(zz > z)
            def _():
                up_copy(zz, xx, piece).start()

            @pl.when(zz < z)
            def _():
                down_copy(zz, xx, piece).start()

            @pl.when(jnp.logical_and(zz == z, xx != x))
            def _():
                across_copy(zz, piece).start()

            return carry

        lax.fori_loop(0, (2 - c) * pieces, one, 0)

    def starts(k):
        return jnp.logical_and(near == 0, k >= 1)

    for load in loads[1:]:
        load.wait()

    def step_of(i, carry):
        k, o = i // 2, i % 2
        zz, xx = nearest(k), (x + o) % 2

        @pl.when(o == 1)
        def _():
            @pl.when(k + 1 < length)
            def _():
                following = nearest(k + 1)
                forward(following, True)

            each_piece(lambda piece: arrival(zz, 1 - x, piece))
            to_partner(zz, 1 - x).start()

        partner_arrival(zz, xx)
        compute(zz, xx)
        answer_copy(zz, xx).start()

        @pl.when(i > 0)
        def _():
            last = nearest((i - 1) // 2)
            last_x = (x + (i - 1) % 2) % 2
            join_partner(last, last_x)

            @pl.when(o == 0)
            def _():
                @pl.when(c == 1)
                def _():
                    all_across(last)

                @pl.when(jnp.logical_and(c == 0, starts(k - 1)))
                def _():
                    chain(last)

        @pl.when(jnp.logical_and(jnp.logical_and(o == 1, c == 1), starts(k - 1)))
        def _():
            chain(nearest(k - 1))

        @pl.when(jnp.logical_and(near == 1, i == 2 * length - 1))
        def _():
            chain(nearest(1))

        return carry

    lax.fori_loop(0, 2 * length, step_of, 0)
    final = nearest(length - 1)
    join_partner(final, 1 - x)

    @pl.when(c == 1)
    def _():
        all_across(final)

    def rest(i, carry):
        k = length - 1 - i

        early = jnp.logical_or(
            jnp.logical_and(starts(k), k < length - 1), jnp.logical_and(near == 1, k == 1)
        )

        @pl.when(jnp.logical_not(early))
        def _():
            chain(nearest(k))

        return carry

    lax.fori_loop(0, length, rest, 0)

    @pl.when(c == 0)
    def _():
        each_piece(lambda piece: take_across(z, piece))

    out_ref[...] = part[z, x]

    for step in range(1, members):
        weights_copy(step).wait_send()

    def drain(zz, carry):
        def one(piece):
            @pl.when(goes_up(zz))
            def _():
                to_above(zz, piece).wait_send()

            @pl.when(goes_down(zz))
            def _():
                to_below(zz, piece).wait_send()

            to_across(zz, piece).wait_send()

            @pl.when(jnp.logical_or(c == 1, zz == z))
            def _():
                across_copy(zz, piece).wait_send()

            @pl.when(zz != z)
            def _():
                up_copy(zz, x, piece).wait_send()

            @pl.when(jnp.logical_and(zz != z, c == 0))
            def _():
                up_copy(zz, 1 - x, piece).wait_send()

        each_piece(one)
        for xx in range(2):
            to_partner(zz, xx).wait_send()
            answer_copy(zz, xx).wait_send()
        return carry

    lax.fori_loop(0, length, drain, 0)


def gathered_plan(tokens, expert_ids, combine, gate_proj, up_proj, down_proj, capacity):
    members = lax.axis_size("ep")
    here, features = tokens.shape
    ff = gate_proj.shape[1]
    length = members // 4
    pieces = 4 if here % 64 == 0 else 1
    experts = jnp.arange(members, dtype=jnp.int32)[:, None, None]
    ids, shares = expert_ids.T[None], combine.T[None]
    mix = jnp.sum(jnp.where(ids == experts, shares, 0.0), axis=1, keepdims=True)
    block = (here, features)
    dma = pltpu.SemaphoreType.DMA
    vmem = lambda *shape: pltpu.VMEM(shape, jnp.bfloat16)
    anywhere = pl.BlockSpec(memory_space=pl.ANY)
    inside = pl.BlockSpec(memory_space=pltpu.VMEM)
    return pl.pallas_call(
        functools.partial(line_kernel, members=members, capacity=capacity, pieces=pieces),
        out_shape=jax.ShapeDtypeStruct(block, jnp.bfloat16),
        in_specs=[anywhere, inside, anywhere, anywhere, anywhere],
        out_specs=inside,
        scratch_shapes=[
            vmem(length, 2, 2, *block),
            pltpu.VMEM((members, 1, here), jnp.float32),
            vmem(features, ff), vmem(features, ff), vmem(ff, features),
            vmem(2 * capacity, features),
            vmem(length, 2, *block), vmem(length, 2, *block), vmem(length, 2, *block),
            vmem(length, *block), vmem(length, 2, *block), vmem(length, 2, *block),
            dma((4,)), dma((length, 2, pieces)), dma((length, pieces)), dma((length, 2)),
            dma((members,)),
            dma((length, 2)), dma((length, pieces)), dma((length, 2, pieces)),
            dma((length, 2, pieces)), dma((length, 2)), dma((members,)), dma((length, 2)),
            dma((length, pieces)), dma((length, 2, pieces)), dma((length, 2, pieces)),
        ],
        compiler_params=pltpu.CompilerParams(
            collective_id=0, has_side_effects=True, vmem_limit_bytes=60 * 1024 * 1024
        ),
    )(tokens, mix, gate_proj, up_proj, down_proj)


def on_device(tokens, expert_ids, combine, gate_weight, up_weight, down_weight):
    members = lax.axis_size("ep")
    tokens_here, fanout = expert_ids.shape
    features = tokens.shape[1]
    capacity = 2 * tokens_here * fanout // members
    received_rows = members * capacity
    if members % 4 == 0 and 2 * capacity >= tokens_here:
        return gathered_plan(
            tokens, expert_ids, combine, gate_weight[0], up_weight[0], down_weight[0], capacity
        )
    flat_ids = expert_ids.reshape(-1)
    onehot = (flat_ids[:, None] == jnp.arange(members, dtype=jnp.int32)[None, :]).astype(jnp.int32)
    running = jnp.cumsum(onehot, axis=0) - onehot
    slot_rank = jnp.sum(running * onehot, axis=1)
    target = flat_ids * capacity + slot_rank
    source_token = jnp.arange(tokens_here * fanout, dtype=jnp.int32) // fanout
    outgoing = (
        jnp.zeros((received_rows, features), jnp.bfloat16).at[target].set(tokens[source_token])
    )
    outgoing = outgoing.reshape(members, capacity, features)
    gate_proj, up_proj, down_proj = (gate_weight[0], up_weight[0], down_weight[0])
    arrived = lax.all_to_all(outgoing, "ep", split_axis=0, concat_axis=0, tiled=True)
    shape_here = arrived.shape
    answers = run_expert_block(
        arrived.reshape(-1, features), gate_proj, up_proj, down_proj
    ).reshape(shape_here)
    returned = lax.all_to_all(answers, "ep", split_axis=0, concat_axis=0, tiled=True)
    selected_experts = (
        returned.reshape(-1, features)[target]
        .astype(jnp.float32)
        .reshape(tokens_here, fanout, features)
    )
    mixture = jnp.sum(selected_experts * combine[:, :, None], axis=1)
    return mixture.astype(jnp.bfloat16)


def solution(mesh):
    in_specs = (
        P(("groups", "ep"), None),
        P(("groups", "ep"), None),
        P(("groups", "ep"), None),
        P("ep", None, None),
        P("ep", None, None),
        P("ep", None, None),
    )
    out_specs = P(("groups", "ep"), None)
    return jax.shard_map(
        on_device, mesh=mesh, in_specs=in_specs, out_specs=out_specs, check_vma=False
    )
```

profile of v0, /device:TPU:0, one launch (start us, length us, event | category | flops | bytes accessed | tf_op | source)
XLA Modules:
  0.0 105.1 jit_solution(16899333361671157024)
XLA Ops:
  0.0 1.3 %select_reduce_fusion = f32[16,128]{1,0:T(8,128)} fusion(f32[4,128]{1,0:T(4,128)} %bitcast.10, s32[4,128]{1,0:T(4,128)} %bitcast.11), kind=kLoop, calls=%fused_computation | loop fusion | flops 22528 | bytes 12288 | tf_op jit(solution)/shard_map/reduce_sum | solution.py:388
  1.3 1.9 %copy.9.tok_hbm = bf16[128,1440]{1,0:T(8,128)(2,1)} copy(bf16[128,1440]{0,1:T(8,128)(2,1)} %param.6) | data formatting | bytes 737280 | tf_op args[0]
  3.2 100.0 %shard_map.64 = bf16[128,1440]{1,0:T(8,128)(2,1)} custom-call(bf16[128,1440]{1,0:T(8,128)(2,1)} %copy.9.tok_hbm, f32[16,1,128]{2,1,0:T(1,128)} %bitcast.9, bf16[1440,1440]{1,0:T(8,128)(2,1)} %bitcast.6, bf16[1440,1440]{1,0:T(8,128)(2,1)} %bitcast.7, bf16[1440,1440]{1,0:T(8,128)(2,1)} %bitcast.8), custom_call_target="tpu_custom_call" | custom-call | tf_op jit(solution)/shard_map/pallas_call | solution.py:394
  103.2 1.9 %copy.10 = bf16[128,1440]{0,1:T(8,128)(2,1)} copy(bf16[128,1440]{1,0:T(8,128)(2,1)} %shard_map.64) | data formatting | bytes 737280 | tf_op jit(solution)/shard_map/pallas_call | solution.py:394
where the time goes:
time: 105 us
  Pallas kernels  100 us (95%)
  local copies, waits for them, and re-layouts  3.81 us (4%)
  other arithmetic  1.3 us (1%)
    pallas_call x1, Pallas kernels, gathered_plan(): pl.pallas_call(functools.partial(line_kernel, members=members, capacity=c...  100 us

commit v1 on v0

v1 whole, which is shorter than its diff:
```python
import functools

import jax
import jax.numpy as jnp
from jax import lax
from jax.experimental import pallas as pl
from jax.experimental.pallas import tpu as pltpu
from jax.sharding import PartitionSpec as P

MESH = pl.DeviceIdType.MESH

alpha_gate = 1.702

SHARES = ((0.0, 0.0, 0.0), (0.67, 0.34, 0.34), 1.0, False)
CHUNKS = (2.4, 1.2)
HOP, ACROSS_CHIP, BLOCK = 1.8, 1.7, 8.0


def run_expert_block(row_block, gate_proj, up_proj, down_proj):
    gate_part = jnp.dot(row_block, gate_proj, preferred_element_type=jnp.float32)
    up_part = jnp.dot(row_block, up_proj, preferred_element_type=jnp.float32)
    hidden = ((up_part + 1.0) * gate_part * jax.nn.sigmoid(alpha_gate * gate_part)).astype(
        jnp.bfloat16
    )
    return jnp.dot(hidden, down_proj, preferred_element_type=jnp.float32).astype(jnp.bfloat16)


class Routes:
    def __init__(self, length, pieces, twin_share, both_share, first=1.0, hold=False):
        self.length, self.pieces = length, pieces
        self.half = (length + 1) // 2
        self.twin_share, self.both_share = twin_share, both_share
        self.first, self.hold = round(first * pieces), hold

    def twin(self, distance, p):
        share = self.twin_share[min(distance, len(self.twin_share)) - 1]
        return p < round(share * self.pieces)

    def both(self, chain, q):
        share = self.both_share[min(chain, len(self.both_share)) - 1]
        return q < round(share * self.pieces)

    def chain(self, u, d):
        return u if d > 0 else self.length - 1 - u

    def exists(self, w, d):
        return 0 <= w + d < self.length

    def late(self, w, p):
        return p >= self.first and w > 0 and w + 1 < self.length

    def neighbour(self, w, d):
        to = w + d
        return (to, False) if to < self.half else (self.length - 1 - to, True)

    def token_moves(self, w, u, col, p):
        if u == w:
            if col == 0:
                out = (1,) if self.late(w, p) else (1, -1)
                return tuple(d for d in out if self.exists(w, d)), True
            return tuple(d for d in (1, -1) if self.exists(w, d) and self.twin(1, p)), False
        d, far = (1, w - u) if u < w else (-1, u - w)
        onward = self.exists(w, d)
        if col == 0:
            return ((d,) if onward else ()), not self.twin(far, p)
        if not self.twin(far, p):
            return (), False
        return ((d,) if onward and self.twin(far + 1, p) else ()), False

    def sum_inputs(self, kind, w, u, col, q):
        if kind == "X":
            return (), False
        if kind == "Z":
            d = 1 if u > w else -1
            return ((d,) if self.exists(w, -d) else ()), not self.both(self.chain(u, d), q)
        chains = tuple(
            d for d in (1, -1)
            if self.exists(w, -d) and (col == 0 or self.both(self.chain(w, d), q))
        )
        return chains, col == 0


def make_plan(routes):
    length, pieces, half = routes.length, routes.pieces, routes.half
    never = 1e9
    wire = BLOCK / pieces
    link, tok, pair_in, ans, cross, chain = {}, {}, {}, {}, {}, {}
    done_at = [dict() for _ in range(half)]

    def push(w, name, now):
        start = max(now, link.get((w, name), 0.0))
        link[w, name] = start + wire
        return start + wire + HOP

    def send_tokens(w, u, col, p, now):
        moves, crosses = routes.token_moves(w, u, col, p)
        for d in moves:
            to, mirrored = routes.neighbour(w, d)
            tok[to, length - 1 - u if mirrored else u, col, p] = push(w, d, now)
        if crosses:
            tok[w, u, 1 - col, p] = push(w, 0, now)
        key = (w, u, col)
        pair_in.setdefault(key, {})[p] = now + ACROSS_CHIP

    def send_sum(kind, w, u, col, q, now):
        if kind == "X" or (kind == "F" and col == 1):
            cross[w, u, q] = push(w, 0, now)
        elif kind == "Z":
            d = 1 if u > w else -1
            to, mirrored = routes.neighbour(w, d)
            key = (to, -d, length - 1 - u) if mirrored else (to, d, u)
            chain[key + (col, q)] = push(w, d, now)

    todo = []
    for w in range(half):
        ops = []
        for u in range(length):
            for col in range(2):
                if (u, col) == (w, 0):
                    ops += [("o", u, 0, p) for p in range(pieces) if routes.late(w, p)]
                else:
                    ops += [("t", u, col, p) for p in range(pieces)]
            for q in range(pieces):
                if u == w:
                    ops += [("F", u, 1, q), ("F", u, 0, q)]
                elif routes.both(routes.chain(u, 1 if u > w else -1), q):
                    ops += [("Z", u, 0, q), ("Z", u, 1, q)]
                else:
                    ops += [("X", u, 1, q), ("Z", u, 0, q)]
        todo.append(ops)

    def ready_at(w, op):
        kind, u, col, p = op
        if kind == "t":
            return tok.get((w, u, col, p), never)
        if kind == "o":
            return never if any(o[:3] == ("t", length - 1, 0) for o in todo[w]) else 0.0
        if routes.hold and (kind == "X" or (kind == "F" and col == 1)) and any(
            o[0] == "t" for o in todo[w]
        ):
            return never
        at = ans.get((w, u, col), never)
        chains, crossing = routes.sum_inputs(kind, w, u, col, p)
        for d in chains:
            at = max(at, chain.get((w, d, u, col, p), never))
        if crossing:
            at = max(at, cross.get((w, u, p), never))
        return at

    rank = {"t": 0, "o": 0, "X": 1, "Z": 2, "F": 3}
    pairs = [
        sorted(((u, col) for u in range(length) for col in range(2)),
               key=lambda k: (abs(k[0] - w), k[1], k[0]))
        for w in range(half)
    ]
    order = [[] for _ in range(half)]
    slots = [{} for _ in range(half)]
    busy = [0.0] * half
    at_slot = [(0, 0)] * half
    running = [None] * half
    for w in range(half):
        for p in range(pieces):
            send_tokens(w, w, 0, p, 0.0)
    steps = 2 * length
    tick, now, end = 0.05, 0.0, [0.0] * half
    while now < 1000 and any(todo):
        for w in range(half):
            if busy[w] > now:
                continue
            if running[w] is not None:
                u, col = running[w]
                ans[w, u, col] = now + ACROSS_CHIP
                running[w] = None
            open_ops, held = [], set()
            for op in todo[w]:
                lane = op[:3]
                if lane in held:
                    continue
                if ready_at(w, op) <= now:
                    open_ops.append(op)
                elif op[0] == "t":
                    held.add(lane)
            i, j = at_slot[w]
            if open_ops:
                op = min(open_ops, key=lambda o: (rank[o[0]], abs(o[1] - w), o[1], o[2], o[3]))
                todo[w].remove(op)
                slots[w].setdefault((i, j), []).append(op)
                kind = op[0]
                busy[w] = now + (0.05 if kind in "to" else 0.4 / pieces + 0.05)
                if kind == "t":
                    send_tokens(w, *op[1:], now)
                elif kind == "o":
                    to, mirrored = routes.neighbour(w, -1)
                    tok[to, length - 1 - w if mirrored else w, 0, op[3]] = push(w, -1, now)
                else:
                    send_sum(kind, w, *op[1:], busy[w])
                end[w] = busy[w]
                continue
            if i < steps:
                if j == 0:
                    got = [
                        k for k in pairs[w]
                        if len(pair_in.get((w,) + k, {})) == pieces
                        and max(pair_in[(w,) + k].values()) <= now
                    ]
                    if not got or now < 2.5:
                        continue
                    pairs[w].remove(got[0])
                    order[w].append(got[0])
                busy[w] = now + CHUNKS[j]
                if j + 1 == len(CHUNKS):
                    running[w] = order[w][-1]
                    at_slot[w] = (i + 1, 0)
                else:
                    at_slot[w] = (i, j + 1)
        now += tick
    return order, slots, end


def grouped(routes, w, ops):
    groups = []
    for kind, u, col, p in ops:
        if kind == "o":
            how = ((-1,), False)
        elif kind == "t":
            how = routes.token_moves(w, u, col, p)
        else:
            how = routes.sum_inputs(kind, w, u, col, p)
        if groups and groups[-1][:4] == [kind, u, col, how] and groups[-1][5] == p:
            groups[-1][5] = p + 1
        else:
            groups.append([kind, u, col, how, p, p + 1])
    return groups


def exchange_kernel(
    ids_ref, share_ref, tok_hbm, gate_hbm, up_hbm, down_hbm, out_ref,
    x_buf, w_out, w_in, rank_buf, gate_w, up_w, down_w, hid, sums, quad, over, flow,
    load_sem, x_s, xp_s, w_s, q_s, sum_s, x_r, xp_r, w_r, q_r, over_r, flow_r,
    *, members, capacity, routes,
):
    length, pieces, half = routes.length, routes.pieces, routes.half
    order, slots, _ = make_plan(routes)
    features, here = tok_hbm.shape
    size = features // pieces
    me = lax.axis_index("ep")
    z, x, c = me // 4, (me // 2) % 2, me % 2
    flip = 2 * z >= length
    at = jnp.where(flip, length - 1 - z, z)

    def member(zz, xx, cc):
        return (zz * 2 + xx) * 2 + cc

    across, partner = member(z, 1 - x, c), member(z, x, 1 - c)
    step_up = jnp.where(flip, -1, 1)

    def beside(d):
        return member(jnp.clip(z + d * step_up, 0, length - 1), x, c)

    def lane(d):
        return jnp.where(flip, 1, 0) if d > 0 else jnp.where(flip, 0, 1)

    def place(u):
        return jnp.where(flip, length - 1 - u, u)

    def column(col):
        return x if col == 0 else 1 - x

    def cut(p, count=1):
        return pl.ds(pl.multiple_of(p * size, size), count * size)

    def send(src, dst, ssem, rsem, to):
        return pltpu.make_async_remote_copy(
            src_ref=src, dst_ref=dst, send_sem=ssem, recv_sem=rsem,
            device_id={"ep": to}, device_id_type=MESH,
        )

    def each(p0, p1, act):
        if p1 - p0 == 1:
            act(p0)
            return

        def one(p, carry):
            act(p)
            return carry

        lax.fori_loop(p0, p1, one, 0)

    loads = [
        pltpu.make_async_copy(tok_hbm, x_buf.at[z, x, c], load_sem.at[0]),
        pltpu.make_async_copy(gate_hbm, gate_w, load_sem.at[1]),
        pltpu.make_async_copy(up_hbm, up_w, load_sem.at[2]),
        pltpu.make_async_copy(down_hbm, down_w, load_sem.at[3]),
    ]
    for load in loads:
        load.start()

    barrier = pltpu.get_barrier_semaphore()
    for step in range(1, members):
        to = lax.rem(me + step, members)
        pl.semaphore_signal(barrier, inc=1, device_id={"ep": to}, device_id_type=MESH)

    expert = lax.broadcasted_iota(jnp.int32, (members, here), 0)
    mix = jnp.zeros((members, here), jnp.float32)
    for k in range(ids_ref.shape[0]):
        mix += jnp.where(ids_ref[k : k + 1, :] == expert, share_ref[k : k + 1, :], 0.0)
    for e in range(members):
        w_out[e] = mix[e : e + 1, :]
    pl.semaphore_wait(barrier, members - 1)

    def weights_copy(step):
        to = lax.rem(me + step, members)
        return send(w_out.at[to], w_in.at[me], w_s.at[step], w_r.at[me], to)

    def weights_arrival(step):
        origin = lax.rem(me + step, members)
        return send(w_out.at[origin], w_in.at[origin], w_s.at[step], w_r.at[origin], origin)

    sent = [[] for _ in range(half)]

    def token_copy(zz, xx, p, way, count=1):
        slot = x_buf.at[zz, xx, c, cut(p, count)]
        number, to = (2, across) if way == 0 else (lane(way), beside(way))
        return send(slot, slot, x_s.at[zz, xx, number], x_r.at[zz, xx, p], to)

    def partner_copy(zz, xx, p=None):
        slot = x_buf.at[zz, xx, c] if p is None else x_buf.at[zz, xx, c, cut(p)]
        return send(slot, slot, xp_s.at[zz, xx], xp_r.at[zz, xx], partner)

    def move_tokens(w, u, col, how, p0, p1, arriving, share=True):
        zz, xx = place(u), column(col)
        ways = tuple(how[0]) + ((0,) if how[1] else ())

        def one(p):
            if arriving:
                token_copy(zz, xx, p, 0).wait_recv()
            for way in ways:
                token_copy(zz, xx, p, way).start()
            if share:
                partner_copy(zz, xx, p).start()

        each(p0, p1, one)
        for way in ways:
            sent[w].append(("t", u, col, way, p1 - p0))

    joins = [{} for _ in range(half)]
    for w in range(half):
        for slot in sorted(slots[w]):
            for kind, u, col, q in slots[w][slot]:
                if kind in "XZF":
                    joins[w].setdefault((u, col), (kind, q))

    def answer_copy(zz, xx):
        return send(
            sums.at[zz, xx, 1 - c], quad.at[zz, xx], q_s.at[zz, xx], q_r.at[zz, xx], partner
        )

    def over_copy(zz, xx, q, count=1):
        return send(
            sums.at[zz, xx, c, cut(q, count)], over.at[zz, cut(q, count)],
            sum_s.at[zz, xx, 0], over_r.at[zz, q], across,
        )

    def flow_copy(zz, xx, q, way, count=1):
        d = lane(way)
        return send(
            sums.at[zz, xx, c, cut(q, count)], flow.at[d, zz, xx, cut(q, count)],
            sum_s.at[zz, xx, 1], flow_r.at[d, zz, xx, q], beside(way),
        )

    def move_sums(kind, w, u, col, how, q0, q1):
        zz, xx = place(u), column(col)
        chains, crossing = how
        if joins[w][u, col] == (kind, q0):
            answer_copy(zz, xx).wait_recv()
        leaves = kind == "X" or (kind == "F" and col == 1)
        onward = 1 if u > w else -1

        def one(q):
            for d in chains:
                flow_copy(zz, xx, q, d).wait_recv()
            if crossing:
                over_copy(zz, xx, q).wait_recv()
            total = sums[zz, xx, c, cut(q)].astype(jnp.float32)
            total += quad[zz, xx, cut(q)].astype(jnp.float32)
            if crossing:
                total += over[zz, cut(q)].astype(jnp.float32)
            for d in chains:
                total += flow[lane(d), zz, xx, cut(q)].astype(jnp.float32)
            total = total.astype(jnp.bfloat16)
            if kind == "F" and col == 0:
                out_ref[cut(q), :] = total
                return
            sums[zz, xx, c, cut(q)] = total
            if leaves:
                over_copy(zz, xx, q).start()
            else:
                flow_copy(zz, xx, q, onward).start()

        each(q0, q1, one)
        if leaves:
            sent[w].append(("x", u, col, 0, q1 - q0))
        elif kind == "Z":
            sent[w].append(("z", u, col, onward, q1 - q0))

    def run_slot(i, j):
        for w in range(half):
            due = [(k, slots[w][k, j]) for k in range(2 * length + 1) if (k, j) in slots[w]]
            due = [(k, ops) for k, ops in due if (k == 2 * length) == (i is None)]
            if not due:
                continue

            @pl.when(at == w)
            def _(w=w, due=due):
                for k, ops in due:

                    def act(ops=ops):
                        for kind, u, col, how, p0, p1 in grouped(routes, w, ops):
                            if kind == "t":
                                move_tokens(w, u, col, how, p0, p1, True)
                            elif kind == "o":
                                move_tokens(w, u, col, how, p0, p1, False, False)
                            else:
                                move_sums(kind, w, u, col, how, p0, p1)

                    if i is None:
                        act()
                    else:
                        pl.when(i == k)(act)

    for step in range(1, members):
        weights_copy(step).start()
    loads[0].wait()
    for w in range(half):

        @pl.when(at == w)
        def _(w=w):
            for _, u, col, how, p0, p1 in grouped(
                routes, w, [("t", w, 0, p) for p in range(pieces)]
            ):
                move_tokens(w, u, col, how, p0, p1, False)

    w_in[me] = w_out[me]
    before = (
        lax.broadcasted_iota(jnp.int32, (here, here), 0)
        < lax.broadcasted_iota(jnp.int32, (here, here), 1)
    ).astype(jnp.bfloat16)
    for step in range(1, members):
        weights_arrival(step).wait_recv()
    weight = jnp.concatenate([w_in[e] for e in range(members)], axis=0)
    named = weight > 0.0
    rank = jnp.dot(
        named.astype(jnp.float32).astype(jnp.bfloat16), before,
        preferred_element_type=jnp.float32,
    )
    rank = jnp.where(named, rank, -1.0)
    for e in range(members):
        rank_buf[e] = rank[e : e + 1, :]
    row_at = lax.broadcasted_iota(jnp.int32, (capacity, here), 0).astype(jnp.float32)

    def pickers(zz, xx):
        picks = []
        for cc in range(2):
            e = member(zz, xx, cc)
            pick = rank_buf[e] == row_at
            picks.append((
                pick.astype(jnp.float32).astype(jnp.bfloat16),
                jnp.where(pick, w_in[e], 0.0).astype(jnp.bfloat16),
            ))
        none = jnp.zeros((capacity, here), jnp.bfloat16)

        def spread(k):
            first = jnp.concatenate([picks[0][k], none], axis=1)
            second = jnp.concatenate([none, picks[1][k]], axis=1)
            return jnp.concatenate([first, second], axis=0)

        return spread(0), spread(1)

    def inner(zz, xx):
        pick, _ = pickers(zz, xx)
        pair = jnp.concatenate([x_buf[zz, xx, 0], x_buf[zz, xx, 1]], axis=1)
        block = lax.dot_general(
            pick, pair, (((1,), (1,)), ((), ())), preferred_element_type=jnp.float32
        ).astype(jnp.bfloat16)
        gate = jnp.dot(block, gate_w[...], preferred_element_type=jnp.float32)
        up = jnp.dot(block, up_w[...], preferred_element_type=jnp.float32)
        hid[...] = ((up + 1.0) * gate * jax.nn.sigmoid(alpha_gate * gate)).astype(jnp.bfloat16)

    def outer(zz, xx):
        _, mixer = pickers(zz, xx)
        answer = jnp.dot(
            hid[...], down_w[...], preferred_element_type=jnp.float32
        ).astype(jnp.bfloat16)
        back = lax.dot_general(
            answer, mixer, (((0,), (0,)), ((), ())), preferred_element_type=jnp.float32
        ).astype(jnp.bfloat16)
        for cc in range(2):
            sums[zz, xx, cc] = back[:, cc * here : (cc + 1) * here]

    def lookup(i, k):
        value = 0
        for w in range(half):
            for n in range(2 * length):
                here_now = jnp.logical_and(at == w, i == n)
                value = jnp.where(here_now, order[w][n][k], value)
        return value

    for load in loads[1:]:
        load.wait()

    def step_of(i, carry):
        run_slot(i, 0)
        zz = place(lookup(i, 0))
        xx = (x + lookup(i, 1)) % 2
        partner_copy(zz, xx).wait_recv()
        inner(zz, xx)
        run_slot(i, 1)
        outer(zz, xx)
        answer_copy(zz, xx).start()
        return carry

    lax.fori_loop(0, 2 * length, step_of, 0)
    run_slot(None, 0)

    for step in range(1, members):
        weights_copy(step).wait_send()
    for w in range(half):

        @pl.when(at == w)
        def _(w=w):
            counts = {}
            for kind, u, col, way, n in sent[w]:
                counts[kind, u, col, way] = counts.get((kind, u, col, way), 0) + n
            for (kind, u, col, way), n in counts.items():
                zz, xx = place(u), column(col)
                if kind == "t":
                    token_copy(zz, xx, 0, way, n).wait_send()
                elif kind == "x":
                    over_copy(zz, xx, 0, n).wait_send()
                else:
                    flow_copy(zz, xx, 0, way, n).wait_send()

    def drain(zz, carry):
        for xx in range(2):
            partner_copy(zz, xx).wait_send()
            answer_copy(zz, xx).wait_send()
        return carry

    lax.fori_loop(0, length, drain, 0)


def gathered_plan(tokens, expert_ids, combine, gate_proj, up_proj, down_proj, capacity):
    members = lax.axis_size("ep")
    here, features = tokens.shape
    ff = gate_proj.shape[1]
    length = members // 4
    pieces = max(n for n in range(1, 7) if features % (16 * n) == 0)
    routes = Routes(length, pieces, *SHARES)
    block = (features, here)
    dma = pltpu.SemaphoreType.DMA
    vmem = lambda *shape: pltpu.VMEM(shape, jnp.bfloat16)
    anywhere = pl.BlockSpec(memory_space=pl.ANY)
    inside = pl.BlockSpec(memory_space=pltpu.VMEM)
    return pl.pallas_call(
        functools.partial(
            exchange_kernel, members=members, capacity=capacity, routes=routes
        ),
        out_shape=jax.ShapeDtypeStruct(block, jnp.bfloat16),
        in_specs=[inside, inside, anywhere, anywhere, anywhere, anywhere],
        out_specs=inside,
        scratch_shapes=[
            vmem(length, 2, 2, *block),
            pltpu.VMEM((members, 1, here), jnp.float32),
            pltpu.VMEM((members, 1, here), jnp.float32),
            pltpu.VMEM((members, 1, here), jnp.float32),
            vmem(features, ff), vmem(features, ff), vmem(ff, features),
            vmem(2 * capacity, ff),
            vmem(length, 2, 2, *block), vmem(length, 2, *block),
            vmem(length, *block), vmem(2, length, 2, *block),
            dma((4,)), dma((length, 2, 3)), dma((length, 2)), dma((members,)),
            dma((length, 2)), dma((length, 2, 2)),
            dma((length, 2, pieces)), dma((length, 2)), dma((members,)), dma((length, 2)),
            dma((length, pieces)), dma((2, length, 2, pieces)),
        ],
        compiler_params=pltpu.CompilerParams(
            collective_id=0, has_side_effects=True, vmem_limit_bytes=60 * 1024 * 1024
        ),
    )(expert_ids.T, combine.T, tokens.T, gate_proj, up_proj, down_proj).T


def on_device(tokens, expert_ids, combine, gate_weight, up_weight, down_weight):
    members = lax.axis_size("ep")
    tokens_here, fanout = expert_ids.shape
    features = tokens.shape[1]
    capacity = 2 * tokens_here * fanout // members
    received_rows = members * capacity
    if members % 4 == 0 and 2 * capacity >= tokens_here:
        return gathered_plan(
            tokens, expert_ids, combine, gate_weight[0], up_weight[0], down_weight[0], capacity
        )
    flat_ids = expert_ids.reshape(-1)
    onehot = (flat_ids[:, None] == jnp.arange(members, dtype=jnp.int32)[None, :]).astype(jnp.int32)
    running = jnp.cumsum(onehot, axis=0) - onehot
    slot_rank = jnp.sum(running * onehot, axis=1)
    target = flat_ids * capacity + slot_rank
    source_token = jnp.arange(tokens_here * fanout, dtype=jnp.int32) // fanout
    outgoing = (
        jnp.zeros((received_rows, features), jnp.bfloat16).at[target].set(tokens[source_token])
    )
    outgoing = outgoing.reshape(members, capacity, features)
    gate_proj, up_proj, down_proj = (gate_weight[0], up_weight[0], down_weight[0])
    arrived = lax.all_to_all(outgoing, "ep", split_axis=0, concat_axis=0, tiled=True)
    shape_here = arrived.shape
    answers = run_expert_block(
        arrived.reshape(-1, features), gate_proj, up_proj, down_proj
    ).reshape(shape_here)
    returned = lax.all_to_all(answers, "ep", split_axis=0, concat_axis=0, tiled=True)
    selected_experts = (
        returned.reshape(-1, features)[target]
        .astype(jnp.float32)
        .reshape(tokens_here, fanout, features)
    )
    mixture = jnp.sum(selected_experts * combine[:, :, None], axis=1)
    return mixture.astype(jnp.bfloat16)


def solution(mesh):
    in_specs = (
        P(("groups", "ep"), None),
        P(("groups", "ep"), None),
        P(("groups", "ep"), None),
        P("ep", None, None),
        P("ep", None, None),
        P("ep", None, None),
    )
    out_specs = P(("groups", "ep"), None)
    return jax.shard_map(
        on_device, mesh=mesh, in_specs=in_specs, out_specs=out_specs, check_vma=False
    )
```

time: 105 us -> 78.1 us (0.74)
  Pallas kernels: 100 us -> 76.1 us
  local copies, waits for them, and re-layouts: 3.81 us -> 1.75 us
  other arithmetic: 1.3 us -> 0 us
    pallas_call x1, Pallas kernels: 100 us -> 76.1 us  [gathered_plan(): pl.pallas_call(functools.partial(exchange_kernel, members=members, capaci...]
    pallas_call x1 -> x0, local copies, waits for them, and re-layouts: 1.91 us -> none  [gathered_plan(): pl.pallas_call(functools.partial(line_kernel, members=members, capacity=c...]
    reduce_sum x1 -> x0, other arithmetic: 1.3 us -> none  [gathered_plan(): mix = jnp.sum(jnp.where(ids == experts, shares, 0.0), axis=1, keepdims=True)]
where the time goes in v1:
time: 78.1 us; the launch traced here: 77.9 us
  Pallas kernels  76.1 us (97%)
  local copies, waits for them, and re-layouts  1.75 us (2%)
    pallas_call x1, Pallas kernels, gathered_plan(): pl.pallas_call(functools.partial(exchange_kernel, members=members, capaci...  76.1 us
    unnamed x1, local copies, waits for them, and re-layouts  1.75 us

profile of v1, /device:TPU:0, one launch (start us, length us, event | category | flops | bytes accessed | tf_op | source)
XLA Modules:
  0.0 77.9 jit_solution(13833094463220646106)
XLA Ops:
  0.0 76.1 %shard_map.64 = bf16[1440,128]{1,0:T(8,128)(2,1)} custom-call(s32[4,128]{1,0:T(4,128)} %bitcast.12, f32[4,128]{1,0:T(4,128)} %bitcast.13, bf16[1440,128]{1,0:T(8,128)(2,1)} %bitcast.11, bf16[1440,1440]{1,0:T(8,128)(2,1)} %bitcast.7, bf16[1440,1440]{1,0:T(8,128)(2,1)} %bitcast.8, bf16[1440,1440]{1,0:T(8,128)(2,1)} %bitcast.9), custom_call_target="tpu_custom_call" | custom-call | tf_op jit(solution)/shard_map/pallas_call | solution.py:564
  76.1 1.7 %copy.8 = bf16[128,1440]{0,1:T(8,128)(2,1)} copy(bf16[128,1440]{0,1:T(8,128)(2,1)} %bitcast.10) | data formatting | bytes 737280

commit v2 on v1

--- a/solution.py
+++ b/solution.py
@@ -11,9 +11,11 @@
 
 alpha_gate = 1.702
 
-SHARES = ((0.0, 0.0, 0.0), (0.67, 0.34, 0.34), 1.0, False)
-CHUNKS = (2.4, 1.2)
-HOP, ACROSS_CHIP, BLOCK = 1.8, 1.7, 8.0
+PIECES = 6
+TWIN, NEAR = ((0.83, 0.5, 0.17), (0.17, 0), (0,)), ((0.67, 0.33, 0.33), (0.67, 0.67), (0,))
+ORDER = ((1.0, 0.33), 1, True, ((15, 10), (0, 15)), ((0, 4, 1, 2, 3, 6, 5, 7), (2, 3, 0, 4, 1, 5, 7, 6)), ((4, 3, 1, 1, 2, 2, 3, 0), (2, 1, 4, 3, 1, 1, 2, 2)))
+CHUNKS = (1.8, 0.9)
+HOP, ACROSS_CHIP, BLOCK = 2.4, 1.6, 8.0
 
 
 def run_expert_block(row_block, gate_proj, up_proj, down_proj):
@@ -26,28 +28,35 @@
 
 
 class Routes:
-    def __init__(self, length, pieces, twin_share, both_share, first=1.0, hold=False):
+    def __init__(self, length, pieces, twin, near, first, crossing, far, after, pairs, urgency):
         self.length, self.pieces = length, pieces
         self.half = (length + 1) // 2
-        self.twin_share, self.both_share = twin_share, both_share
-        self.first, self.hold = round(first * pieces), hold
-
-    def twin(self, distance, p):
-        share = self.twin_share[min(distance, len(self.twin_share)) - 1]
-        return p < round(share * self.pieces)
-
-    def both(self, chain, q):
-        share = self.both_share[min(chain, len(self.both_share)) - 1]
-        return q < round(share * self.pieces)
-
-    def chain(self, u, d):
-        return u if d > 0 else self.length - 1 - u
+        self.shares = twin, near
+        self.first, self.crossing, self.far = first, crossing, far
+        self.after, self.pairs, self.urgency = after, pairs, urgency
+
+    def within(self, which, u, w, distance, p):
+        if u >= self.half:
+            u, w = self.length - 1 - u, self.length - 1 - w
+        kind = 0 if u == 0 else 1 if w > u else 2
+        shares = self.shares[which][kind]
+        return p < shares[min(distance, len(shares)) - 1] * self.pieces - 0.5
+
+    def twin(self, u, w, distance, p):
+        return self.within(0, u, w, distance, p)
+
+    def near(self, u, w, distance, q):
+        return self.within(1, u, w, distance, q)
 
     def exists(self, w, d):
         return 0 <= w + d < self.length
 
-    def late(self, w, p):
-        return p >= self.first and w > 0 and w + 1 < self.length
+    def late(self, w, p, d):
+        share = self.first[d < 0]
+        return p >= share * self.pieces - 0.5 and w > 0 and w + 1 < self.length
+
+    def crosses_late(self, p):
+        return p >= self.crossing * self.pieces - 0.5
 
     def neighbour(self, w, d):
         to = w + d
@@ -55,27 +64,29 @@
 
     def token_moves(self, w, u, col, p):
         if u == w:
+            ways = tuple(d for d in (1, -1) if self.exists(w, d))
             if col == 0:
-                out = (1,) if self.late(w, p) else (1, -1)
-                return tuple(d for d in out if self.exists(w, d)), True
-            return tuple(d for d in (1, -1) if self.exists(w, d) and self.twin(1, p)), False
+                early = tuple(d for d in ways if not self.late(w, p, d))
+                return early, not self.crosses_late(p)
+            return tuple(d for d in ways if self.twin(w, w + d, 1, p)), False
         d, far = (1, w - u) if u < w else (-1, u - w)
         onward = self.exists(w, d)
         if col == 0:
-            return ((d,) if onward else ()), not self.twin(far, p)
-        if not self.twin(far, p):
+            return ((d,) if onward else ()), not self.twin(u, w, far, p)
+        if not self.twin(u, w, far, p):
             return (), False
-        return ((d,) if onward and self.twin(far + 1, p) else ()), False
+        return ((d,) if onward and self.twin(u, w, far + 1, p) else ()), False
 
     def sum_inputs(self, kind, w, u, col, q):
         if kind == "X":
             return (), False
         if kind == "Z":
-            d = 1 if u > w else -1
-            return ((d,) if self.exists(w, -d) else ()), not self.both(self.chain(u, d), q)
+            d, away = (1, u - w) if u > w else (-1, w - u)
+            chains = self.exists(w, -d) and (col == 0 or self.near(u, w, away + 1, q))
+            return ((d,) if chains else ()), not self.near(u, w, away, q)
         chains = tuple(
             d for d in (1, -1)
-            if self.exists(w, -d) and (col == 0 or self.both(self.chain(w, d), q))
+            if self.exists(w, -d) and (col == 0 or self.near(w, w - d, 1, q))
         )
         return chains, col == 0
 
@@ -117,13 +128,15 @@
         for u in range(length):
             for col in range(2):
                 if (u, col) == (w, 0):
-                    ops += [("o", u, 0, p) for p in range(pieces) if routes.late(w, p)]
+                    ops += [("o", u, 0, p) for p in range(pieces) if routes.late(w, p, -1)]
+                    ops += [("v", u, 0, p) for p in range(pieces) if routes.late(w, p, 1)]
+                    ops += [("c", u, 0, p) for p in range(pieces) if routes.crosses_late(p)]
                 else:
                     ops += [("t", u, col, p) for p in range(pieces)]
             for q in range(pieces):
                 if u == w:
                     ops += [("F", u, 1, q), ("F", u, 0, q)]
-                elif routes.both(routes.chain(u, 1 if u > w else -1), q):
+                elif routes.near(u, w, abs(u - w), q):
                     ops += [("Z", u, 0, q), ("Z", u, 1, q)]
                 else:
                     ops += [("X", u, 1, q), ("Z", u, 0, q)]
@@ -135,11 +148,16 @@
             return tok.get((w, u, col, p), never)
         if kind == "o":
             return never if any(o[:3] == ("t", length - 1, 0) for o in todo[w]) else 0.0
-        if routes.hold and (kind == "X" or (kind == "F" and col == 1)) and any(
-            o[0] == "t" for o in todo[w]
-        ):
-            return never
+        if kind == "v":
+            return never if any(o[0] == "t" and o[1] < w and o[2] == 0 for o in todo[w]) else 0.0
+        if kind == "c":
+            waiting = any(
+                o[0] == "t" and routes.token_moves(w, *o[1:])[1] for o in todo[w]
+            )
+            return never if waiting else 0.0
         at = ans.get((w, u, col), never)
+        if kind == "X" or (kind == "F" and col == 1):
+            at = max(at, routes.after[w][kind == "F"])
         chains, crossing = routes.sum_inputs(kind, w, u, col, p)
         for d in chains:
             at = max(at, chain.get((w, d, u, col, p), never))
@@ -147,12 +165,24 @@
             at = max(at, cross.get((w, u, p), never))
         return at
 
-    rank = {"t": 0, "o": 0, "X": 1, "Z": 2, "F": 3}
-    pairs = [
-        sorted(((u, col) for u in range(length) for col in range(2)),
-               key=lambda k: (abs(k[0] - w), k[1], k[0]))
-        for w in range(half)
-    ]
+    pairs = []
+    for w in range(half):
+        wanted = sorted(
+            ((u, col) for u in range(length) for col in range(2)),
+            key=lambda k: (abs(k[0] - w), k[1], k[0]),
+        )
+        if length == len(routes.pairs[w]) // 2:
+            wanted = [(n // 2, n % 2) for n in routes.pairs[w]]
+        pairs.append(wanted)
+
+    def precedence(w, op):
+        kind, u, col, p = op
+        if kind in "tocv":
+            return -1, (-1 if routes.far else 1) * abs(u - w), u, col, p
+        n = 2 * u + col
+        rank = routes.urgency[w][n] if 2 * length == len(routes.urgency[w]) else abs(u - w)
+        return rank, kind != "X", u, col, p
+
     order = [[] for _ in range(half)]
     slots = [{} for _ in range(half)]
     busy = [0.0] * half
@@ -162,7 +192,7 @@
         for p in range(pieces):
             send_tokens(w, w, 0, p, 0.0)
     steps = 2 * length
-    tick, now, end = 0.05, 0.0, [0.0] * half
+    tick, now, end = 0.1, 0.0, [0.0] * half
     while now < 1000 and any(todo):
         for w in range(half):
             if busy[w] > now:
@@ -182,16 +212,19 @@
                     held.add(lane)
             i, j = at_slot[w]
             if open_ops:
-                op = min(open_ops, key=lambda o: (rank[o[0]], abs(o[1] - w), o[1], o[2], o[3]))
+                op = min(open_ops, key=lambda o: precedence(w, o))
                 todo[w].remove(op)
                 slots[w].setdefault((i, j), []).append(op)
                 kind = op[0]
-                busy[w] = now + (0.05 if kind in "to" else 0.4 / pieces + 0.05)
+                busy[w] = now + (0.05 if kind in "tocv" else 0.4 / pieces + 0.05)
                 if kind == "t":
                     send_tokens(w, *op[1:], now)
-                elif kind == "o":
-                    to, mirrored = routes.neighbour(w, -1)
-                    tok[to, length - 1 - w if mirrored else w, 0, op[3]] = push(w, -1, now)
+                elif kind in "ov":
+                    way = -1 if kind == "o" else 1
+                    to, mirrored = routes.neighbour(w, way)
+                    tok[to, length - 1 - w if mirrored else w, 0, op[3]] = push(w, way, now)
+                elif kind == "c":
+                    tok[w, w, 1, op[3]] = push(w, 0, now)
                 else:
                     send_sum(kind, w, *op[1:], busy[w])
                 end[w] = busy[w]
@@ -220,8 +253,8 @@
 def grouped(routes, w, ops):
     groups = []
     for kind, u, col, p in ops:
-        if kind == "o":
-            how = ((-1,), False)
+        if kind in "ocv":
+            how = {"o": ((-1,), False), "v": ((1,), False), "c": ((), True)}[kind]
         elif kind == "t":
             how = routes.token_moves(w, u, col, p)
         else:
@@ -418,7 +451,7 @@
                         for kind, u, col, how, p0, p1 in grouped(routes, w, ops):
                             if kind == "t":
                                 move_tokens(w, u, col, how, p0, p1, True)
-                            elif kind == "o":
+                            elif kind in "ocv":
                                 move_tokens(w, u, col, how, p0, p1, False, False)
                             else:
                                 move_sums(kind, w, u, col, how, p0, p1)
@@ -554,8 +587,8 @@
     here, features = tokens.shape
     ff = gate_proj.shape[1]
     length = members // 4
-    pieces = max(n for n in range(1, 7) if features % (16 * n) == 0)
-    routes = Routes(length, pieces, *SHARES)
+    pieces = max(n for n in range(1, PIECES + 1) if features % (16 * n) == 0)
+    routes = Routes(length, pieces, TWIN, NEAR, *ORDER)
     block = (features, here)
     dma = pltpu.SemaphoreType.DMA
     vmem = lambda *shape: pltpu.VMEM(shape, jnp.bfloat16)

time: 78.1 us -> 68.3 us (0.87)
  Pallas kernels: 76.1 us -> 66.4 us
    pallas_call x1, Pallas kernels: 76.1 us -> 66.4 us  [gathered_plan(): pl.pallas_call(functools.partial(exchange_kernel, members=members, capaci...]
where the time goes in v2:
time: 68.3 us; the launch traced here: 68.2 us
  Pallas kernels  66.4 us (97%)
  local copies, waits for them, and re-layouts  1.75 us (3%)
    pallas_call x1, Pallas kernels, gathered_plan(): pl.pallas_call(functools.partial(exchange_kernel, members=members, capaci...  66.4 us
    unnamed x1, local copies, waits for them, and re-layouts  1.75 us

profile of v2, /device:TPU:0, one launch (start us, length us, event | category | flops | bytes accessed | tf_op | source)
XLA Modules:
  0.0 68.2 jit_solution(9354796409078637237)
XLA Ops:
  0.0 66.4 %shard_map.64 = bf16[1440,128]{1,0:T(8,128)(2,1)} custom-call(s32[4,128]{1,0:T(4,128)} %bitcast.12, f32[4,128]{1,0:T(4,128)} %bitcast.13, bf16[1440,128]{1,0:T(8,128)(2,1)} %bitcast.11, bf16[1440,1440]{1,0:T(8,128)(2,1)} %bitcast.7, bf16[1440,1440]{1,0:T(8,128)(2,1)} %bitcast.8, bf16[1440,1440]{1,0:T(8,128)(2,1)} %bitcast.9), custom_call_target="tpu_custom_call" | custom-call | tf_op jit(solution)/shard_map/pallas_call | solution.py:597
  66.4 1.7 %copy.8 = bf16[128,1440]{0,1:T(8,128)(2,1)} copy(bf16[128,1440]{0,1:T(8,128)(2,1)} %bitcast.10) | data formatting | bytes 737280

commit v3 on v2

--- a/solution.py
+++ b/solution.py
@@ -11,9 +11,9 @@
 
 alpha_gate = 1.702
 
-PIECES = 6
-TWIN, NEAR = ((0.83, 0.5, 0.17), (0.17, 0), (0,)), ((0.67, 0.33, 0.33), (0.67, 0.67), (0,))
-ORDER = ((1.0, 0.33), 1, True, ((15, 10), (0, 15)), ((0, 4, 1, 2, 3, 6, 5, 7), (2, 3, 0, 4, 1, 5, 7, 6)), ((4, 3, 1, 1, 2, 2, 3, 0), (2, 1, 4, 3, 1, 1, 2, 2)))
+PIECES, PARTS = 7, 6
+TWIN, NEAR = ((0.67, 0.5, 0.17), (0.17, 0), (0,)), ((0.83, 0.33, 0.33), (0.67, 0.67), (0,))
+ORDER = ((1.0, 0.33), 1, True, ((0, 5), (0, 0)), ((0, 1, 4, 2, 3, 6, 5, 7), (2, 3, 0, 4, 1, 5, 7, 6)), ((1, 4, 1, 1, 2, 2, 3, 3), (2, 1, 4, 4, 3, 1, 2, 2)))
 CHUNKS = (1.8, 0.9)
 HOP, ACROSS_CHIP, BLOCK = 2.4, 1.6, 8.0
 
@@ -28,8 +28,8 @@
 
 
 class Routes:
-    def __init__(self, length, pieces, twin, near, first, crossing, far, after, pairs, urgency):
-        self.length, self.pieces = length, pieces
+    def __init__(self, length, pieces, parts, twin, near, first, crossing, far, after, pairs, urgency):
+        self.length, self.pieces, self.parts = length, pieces, parts
         self.half = (length + 1) // 2
         self.shares = twin, near
         self.first, self.crossing, self.far = first, crossing, far
@@ -40,7 +40,8 @@
             u, w = self.length - 1 - u, self.length - 1 - w
         kind = 0 if u == 0 else 1 if w > u else 2
         shares = self.shares[which][kind]
-        return p < shares[min(distance, len(shares)) - 1] * self.pieces - 0.5
+        count = self.parts if which else self.pieces
+        return p < shares[min(distance, len(shares)) - 1] * count - 0.5
 
     def twin(self, u, w, distance, p):
         return self.within(0, u, w, distance, p)
@@ -93,12 +94,13 @@
 
 def make_plan(routes):
     length, pieces, half = routes.length, routes.pieces, routes.half
+    parts = routes.parts
     never = 1e9
-    wire = BLOCK / pieces
+    token_wire, sum_wire = BLOCK / pieces, BLOCK / parts
     link, tok, pair_in, ans, cross, chain = {}, {}, {}, {}, {}, {}
     done_at = [dict() for _ in range(half)]
 
-    def push(w, name, now):
+    def push(w, name, now, wire=token_wire):
         start = max(now, link.get((w, name), 0.0))
         link[w, name] = start + wire
         return start + wire + HOP
@@ -115,12 +117,12 @@
 
     def send_sum(kind, w, u, col, q, now):
         if kind == "X" or (kind == "F" and col == 1):
-            cross[w, u, q] = push(w, 0, now)
+            cross[w, u, q] = push(w, 0, now, sum_wire)
         elif kind == "Z":
             d = 1 if u > w else -1
             to, mirrored = routes.neighbour(w, d)
             key = (to, -d, length - 1 - u) if mirrored else (to, d, u)
-            chain[key + (col, q)] = push(w, d, now)
+            chain[key + (col, q)] = push(w, d, now, sum_wire)
 
     todo = []
     for w in range(half):
@@ -133,7 +135,7 @@
                     ops += [("c", u, 0, p) for p in range(pieces) if routes.crosses_late(p)]
                 else:
                     ops += [("t", u, col, p) for p in range(pieces)]
-            for q in range(pieces):
+            for q in range(parts):
                 if u == w:
                     ops += [("F", u, 1, q), ("F", u, 0, q)]
                 elif routes.near(u, w, abs(u - w), q):
@@ -216,7 +218,7 @@
                 todo[w].remove(op)
                 slots[w].setdefault((i, j), []).append(op)
                 kind = op[0]
-                busy[w] = now + (0.05 if kind in "tocv" else 0.4 / pieces + 0.05)
+                busy[w] = now + (0.05 if kind in "tocv" else 0.4 / parts + 0.05)
                 if kind == "t":
                     send_tokens(w, *op[1:], now)
                 elif kind in "ov":
@@ -267,15 +269,16 @@
 
 
 def exchange_kernel(
-    ids_ref, share_ref, tok_hbm, gate_hbm, up_hbm, down_hbm, out_ref,
-    x_buf, w_out, w_in, rank_buf, gate_w, up_w, down_w, hid, sums, quad, over, flow,
-    load_sem, x_s, xp_s, w_s, q_s, sum_s, x_r, xp_r, w_r, q_r, over_r, flow_r,
+    ids_hbm, share_hbm, tok_hbm, gate_hbm, up_hbm, down_hbm, out_ref,
+    ids_ref, share_ref, x_buf, gate_w, up_w, down_w, hid, mixer, sums, quad, over, flow,
+    load_sem, x_s, xp_s, q_s, sum_s, x_r, xp_r, q_r, over_r, flow_r,
     *, members, capacity, routes,
 ):
     length, pieces, half = routes.length, routes.pieces, routes.half
     order, slots, _ = make_plan(routes)
     features, here = tok_hbm.shape
-    size = features // pieces
+    deep = x_buf.shape[3]
+    size, span = deep // pieces, features // routes.parts
     me = lax.axis_index("ep")
     z, x, c = me // 4, (me // 2) % 2, me % 2
     flip = 2 * z >= length
@@ -302,6 +305,9 @@
     def cut(p, count=1):
         return pl.ds(pl.multiple_of(p * size, size), count * size)
 
+    def stretch(q, count=1):
+        return pl.ds(pl.multiple_of(q * span, span), count * span)
+
     def send(src, dst, ssem, rsem, to):
         return pltpu.make_async_remote_copy(
             src_ref=src, dst_ref=dst, send_sem=ssem, recv_sem=rsem,
@@ -320,34 +326,44 @@
         lax.fori_loop(p0, p1, one, 0)
 
     loads = [
-        pltpu.make_async_copy(tok_hbm, x_buf.at[z, x, c], load_sem.at[0]),
+        pltpu.make_async_copy(tok_hbm, x_buf.at[z, x, c, pl.ds(0, features)], load_sem.at[0]),
         pltpu.make_async_copy(gate_hbm, gate_w, load_sem.at[1]),
         pltpu.make_async_copy(up_hbm, up_w, load_sem.at[2]),
         pltpu.make_async_copy(down_hbm, down_w, load_sem.at[3]),
     ]
-    for load in loads:
+    lists = [
+        pltpu.make_async_copy(ids_hbm, ids_ref, load_sem.at[4]),
+        pltpu.make_async_copy(share_hbm, share_ref, load_sem.at[5]),
+    ]
+    for load in lists + loads:
         load.start()
 
     barrier = pltpu.get_barrier_semaphore()
-    for step in range(1, members):
-        to = lax.rem(me + step, members)
+    above, below = z < length - 1, z > 0
+
+    def greet(to):
         pl.semaphore_signal(barrier, inc=1, device_id={"ep": to}, device_id_type=MESH)
 
-    expert = lax.broadcasted_iota(jnp.int32, (members, here), 0)
-    mix = jnp.zeros((members, here), jnp.float32)
+    greet(partner)
+    greet(across)
+
+    @pl.when(above)
+    def _():
+        greet(member(z + 1, x, c))
+
+    @pl.when(below)
+    def _():
+        greet(member(z - 1, x, c))
+
+    for load in lists:
+        load.wait()
+    table = deep - features
+    expert = lax.broadcasted_iota(jnp.int32, (table, here), 0)
+    mix = jnp.zeros((table, here), jnp.float32)
     for k in range(ids_ref.shape[0]):
         mix += jnp.where(ids_ref[k : k + 1, :] == expert, share_ref[k : k + 1, :], 0.0)
-    for e in range(members):
-        w_out[e] = mix[e : e + 1, :]
-    pl.semaphore_wait(barrier, members - 1)
-
-    def weights_copy(step):
-        to = lax.rem(me + step, members)
-        return send(w_out.at[to], w_in.at[me], w_s.at[step], w_r.at[me], to)
-
-    def weights_arrival(step):
-        origin = lax.rem(me + step, members)
-        return send(w_out.at[origin], w_in.at[origin], w_s.at[step], w_r.at[origin], origin)
+    x_buf[z, x, c, features:deep, :] = mix.astype(jnp.bfloat16)
+    pl.semaphore_wait(barrier, 2 + jnp.where(above, 1, 0) + jnp.where(below, 1, 0))
 
     sent = [[] for _ in range(half)]
 
@@ -390,14 +406,14 @@
 
     def over_copy(zz, xx, q, count=1):
         return send(
-            sums.at[zz, xx, c, cut(q, count)], over.at[zz, cut(q, count)],
+            sums.at[zz, xx, c, stretch(q, count)], over.at[zz, stretch(q, count)],
             sum_s.at[zz, xx, 0], over_r.at[zz, q], across,
         )
 
     def flow_copy(zz, xx, q, way, count=1):
         d = lane(way)
         return send(
-            sums.at[zz, xx, c, cut(q, count)], flow.at[d, zz, xx, cut(q, count)],
+            sums.at[zz, xx, c, stretch(q, count)], flow.at[d, zz, xx, stretch(q, count)],
             sum_s.at[zz, xx, 1], flow_r.at[d, zz, xx, q], beside(way),
         )
 
@@ -414,17 +430,17 @@
                 flow_copy(zz, xx, q, d).wait_recv()
             if crossing:
                 over_copy(zz, xx, q).wait_recv()
-            total = sums[zz, xx, c, cut(q)].astype(jnp.float32)
-            total += quad[zz, xx, cut(q)].astype(jnp.float32)
+            total = sums[zz, xx, c, stretch(q)].astype(jnp.float32)
+            total += quad[zz, xx, stretch(q)].astype(jnp.float32)
             if crossing:
-                total += over[zz, cut(q)].astype(jnp.float32)
+                total += over[zz, stretch(q)].astype(jnp.float32)
             for d in chains:
-                total += flow[lane(d), zz, xx, cut(q)].astype(jnp.float32)
+                total += flow[lane(d), zz, xx, stretch(q)].astype(jnp.float32)
             total = total.astype(jnp.bfloat16)
             if kind == "F" and col == 0:
-                out_ref[cut(q), :] = total
+                out_ref[stretch(q), :] = total
                 return
-            sums[zz, xx, c, cut(q)] = total
+            sums[zz, xx, c, stretch(q)] = total
             if leaves:
                 over_copy(zz, xx, q).start()
             else:
@@ -461,8 +477,6 @@
                     else:
                         pl.when(i == k)(act)
 
-    for step in range(1, members):
-        weights_copy(step).start()
     loads[0].wait()
     for w in range(half):
 
@@ -473,34 +487,32 @@
             ):
                 move_tokens(w, u, col, how, p0, p1, False)
 
-    w_in[me] = w_out[me]
     before = (
         lax.broadcasted_iota(jnp.int32, (here, here), 0)
         < lax.broadcasted_iota(jnp.int32, (here, here), 1)
     ).astype(jnp.bfloat16)
-    for step in range(1, members):
-        weights_arrival(step).wait_recv()
-    weight = jnp.concatenate([w_in[e] for e in range(members)], axis=0)
-    named = weight > 0.0
-    rank = jnp.dot(
-        named.astype(jnp.float32).astype(jnp.bfloat16), before,
-        preferred_element_type=jnp.float32,
-    )
-    rank = jnp.where(named, rank, -1.0)
-    for e in range(members):
-        rank_buf[e] = rank[e : e + 1, :]
     row_at = lax.broadcasted_iota(jnp.int32, (capacity, here), 0).astype(jnp.float32)
 
     def pickers(zz, xx):
+        weights = []
+        for cc in range(2):
+            listed = x_buf[zz, xx, cc, features:deep, :].astype(jnp.float32)
+            weights.append(jnp.sum(jnp.where(expert == me, listed, 0.0), axis=0, keepdims=True))
+        line = lax.broadcasted_iota(jnp.int32, (16, here), 0)
+        flags = jnp.where(line == 0, weights[0], jnp.where(line == 1, weights[1], 0.0)) > 0.0
+        rank = jnp.dot(
+            flags.astype(jnp.float32).astype(jnp.bfloat16), before,
+            preferred_element_type=jnp.float32,
+        )
+        none = jnp.zeros((capacity, here), jnp.bfloat16)
         picks = []
         for cc in range(2):
-            e = member(zz, xx, cc)
-            pick = rank_buf[e] == row_at
+            named = weights[cc] > 0.0
+            pick = jnp.where(named, rank[cc : cc + 1, :], -1.0) == row_at
             picks.append((
                 pick.astype(jnp.float32).astype(jnp.bfloat16),
-                jnp.where(pick, w_in[e], 0.0).astype(jnp.bfloat16),
+                jnp.where(pick, weights[cc], 0.0).astype(jnp.bfloat16),
             ))
-        none = jnp.zeros((capacity, here), jnp.bfloat16)
 
         def spread(k):
             first = jnp.concatenate([picks[0][k], none], axis=1)
@@ -510,8 +522,10 @@
         return spread(0), spread(1)
 
     def inner(zz, xx):
-        pick, _ = pickers(zz, xx)
-        pair = jnp.concatenate([x_buf[zz, xx, 0], x_buf[zz, xx, 1]], axis=1)
+        pick, mixer[...] = pickers(zz, xx)
+        pair = jnp.concatenate(
+            [x_buf[zz, xx, 0, :features, :], x_buf[zz, xx, 1, :features, :]], axis=1
+        )
         block = lax.dot_general(
             pick, pair, (((1,), (1,)), ((), ())), preferred_element_type=jnp.float32
         ).astype(jnp.bfloat16)
@@ -520,12 +534,11 @@
         hid[...] = ((up + 1.0) * gate * jax.nn.sigmoid(alpha_gate * gate)).astype(jnp.bfloat16)
 
     def outer(zz, xx):
-        _, mixer = pickers(zz, xx)
         answer = jnp.dot(
             hid[...], down_w[...], preferred_element_type=jnp.float32
         ).astype(jnp.bfloat16)
         back = lax.dot_general(
-            answer, mixer, (((0,), (0,)), ((), ())), preferred_element_type=jnp.float32
+            answer, mixer[...], (((0,), (0,)), ((), ())), preferred_element_type=jnp.float32
         ).astype(jnp.bfloat16)
         for cc in range(2):
             sums[zz, xx, cc] = back[:, cc * here : (cc + 1) * here]
@@ -555,8 +568,6 @@
     lax.fori_loop(0, 2 * length, step_of, 0)
     run_slot(None, 0)
 
-    for step in range(1, members):
-        weights_copy(step).wait_send()
     for w in range(half):
 
         @pl.when(at == w)
@@ -587,8 +598,10 @@
     here, features = tokens.shape
     ff = gate_proj.shape[1]
     length = members // 4
-    pieces = max(n for n in range(1, PIECES + 1) if features % (16 * n) == 0)
-    routes = Routes(length, pieces, TWIN, NEAR, *ORDER)
+    deep = features + -(-members // 16) * 16
+    pieces = max(n for n in range(1, PIECES + 1) if deep % (16 * n) == 0)
+    parts = max(n for n in range(1, PARTS + 1) if features % (16 * n) == 0)
+    routes = Routes(length, pieces, parts, TWIN, NEAR, *ORDER)
     block = (features, here)
     dma = pltpu.SemaphoreType.DMA
     vmem = lambda *shape: pltpu.VMEM(shape, jnp.bfloat16)
@@ -599,21 +612,20 @@
             exchange_kernel, members=members, capacity=capacity, routes=routes
         ),
         out_shape=jax.ShapeDtypeStruct(block, jnp.bfloat16),
-        in_specs=[inside, inside, anywhere, anywhere, anywhere, anywhere],
+        in_specs=[anywhere, anywhere, anywhere, anywhere, anywhere, anywhere],
         out_specs=inside,
         scratch_shapes=[
-            vmem(length, 2, 2, *block),
-            pltpu.VMEM((members, 1, here), jnp.float32),
-            pltpu.VMEM((members, 1, here), jnp.float32),
-            pltpu.VMEM((members, 1, here), jnp.float32),
+            pltpu.VMEM(expert_ids.shape[::-1], jnp.int32),
+            pltpu.VMEM(combine.shape[::-1], jnp.float32),
+            vmem(length, 2, 2, deep, here),
             vmem(features, ff), vmem(features, ff), vmem(ff, features),
-            vmem(2 * capacity, ff),
+            vmem(2 * capacity, ff), vmem(2 * capacity, 2 * here),
             vmem(length, 2, 2, *block), vmem(length, 2, *block),
             vmem(length, *block), vmem(2, length, 2, *block),
-            dma((4,)), dma((length, 2, 3)), dma((length, 2)), dma((members,)),
+            dma((6,)), dma((length, 2, 3)), dma((length, 2)),
             dma((length, 2)), dma((length, 2, 2)),
-            dma((length, 2, pieces)), dma((length, 2)), dma((members,)), dma((length, 2)),
-            dma((length, pieces)), dma((2, length, 2, pieces)),
+            dma((length, 2, pieces)), dma((length, 2)), dma((length, 2)),
+            dma((length, parts)), dma((2, length, 2, parts)),
         ],
         compiler_params=pltpu.CompilerParams(
             collective_id=0, has_side_effects=True, vmem_limit_bytes=60 * 1024 * 1024

time: 68.3 us -> 66.2 us (0.969)
  Pallas kernels: 66.4 us -> 64.3 us
    pallas_call x1, Pallas kernels: 66.4 us -> 64.3 us  [gathered_plan(): pl.pallas_call(functools.partial(exchange_kernel, members=members, capaci...]
where the time goes in v3:
time: 66.2 us; the launch traced here: 66.1 us
  Pallas kernels  64.3 us (97%)
  local copies, waits for them, and re-layouts  1.75 us (3%)
    pallas_call x1, Pallas kernels, gathered_plan(): pl.pallas_call(functools.partial(exchange_kernel, members=members, capaci...  64.3 us
    unnamed x1, local copies, waits for them, and re-layouts  1.75 us

profile of v3, /device:TPU:0, one launch (start us, length us, event | category | flops | bytes accessed | tf_op | source)
XLA Modules:
  0.0 66.1 jit_solution(6957369490991427133)
XLA Ops:
  0.0 64.3 %shard_map.64 = bf16[1440,128]{1,0:T(8,128)(2,1)} custom-call(s32[4,128]{1,0:T(4,128)} %bitcast.12, f32[4,128]{1,0:T(4,128)} %bitcast.13, bf16[1440,128]{1,0:T(8,128)(2,1)} %bitcast.11, bf16[1440,1440]{1,0:T(8,128)(2,1)} %bitcast.7, bf16[1440,1440]{1,0:T(8,128)(2,1)} %bitcast.8, bf16[1440,1440]{1,0:T(8,128)(2,1)} %bitcast.9), custom_call_target="tpu_custom_call" | custom-call | tf_op jit(solution)/shard_map/pallas_call | solution.py:610
  64.3 1.7 %copy.8 = bf16[128,1440]{0,1:T(8,128)(2,1)} copy(bf16[128,1440]{0,1:T(8,128)(2,1)} %bitcast.10) | data formatting | bytes 737280

commit v4 on v3

--- a/solution.py
+++ b/solution.py
@@ -11,9 +11,9 @@
 
 alpha_gate = 1.702
 
-PIECES, PARTS = 7, 6
-TWIN, NEAR = ((0.67, 0.5, 0.17), (0.17, 0), (0,)), ((0.83, 0.33, 0.33), (0.67, 0.67), (0,))
-ORDER = ((1.0, 0.33), 1, True, ((0, 5), (0, 0)), ((0, 1, 4, 2, 3, 6, 5, 7), (2, 3, 0, 4, 1, 5, 7, 6)), ((1, 4, 1, 1, 2, 2, 3, 3), (2, 1, 4, 4, 3, 1, 2, 2)))
+PIECES, PARTS = 7, 9
+TWIN, NEAR = ((0.56, 0.44, 0), (0, 0), (0,)), ((0.33, 0.33, 0.33), (0.22, 0.11), (0.89,))
+ORDER = ((0.33, 1.0), 0.56, True, ((8, 37), (5, 0)), ((0, 3, 4, 7, 2, 6, 1, 5), (2, 6, 5, 0, 3, 1, 7, 4)), ((0, 0, 3, 0, 2, 4, 3, 1), (2, 1, 0, 3, 4, 3, 2, 4)), (12, 12))
 CHUNKS = (1.8, 0.9)
 HOP, ACROSS_CHIP, BLOCK = 2.4, 1.6, 8.0
 
@@ -28,12 +28,13 @@
 
 
 class Routes:
-    def __init__(self, length, pieces, parts, twin, near, first, crossing, far, after, pairs, urgency):
+    def __init__(self, length, pieces, parts, twin, near, first, crossing, far, after, pairs, urgency, quota):
         self.length, self.pieces, self.parts = length, pieces, parts
         self.half = (length + 1) // 2
         self.shares = twin, near
         self.first, self.crossing, self.far = first, crossing, far
         self.after, self.pairs, self.urgency = after, pairs, urgency
+        self.quota = quota
 
     def within(self, which, u, w, distance, p):
         if u >= self.half:
@@ -213,6 +214,17 @@
                 elif op[0] == "t":
                     held.add(lane)
             i, j = at_slot[w]
+            got = []
+            if i < steps and j == 0 and now >= 2.5:
+                got = [
+                    k for k in pairs[w]
+                    if len(pair_in.get((w,) + k, {})) == pieces
+                    and max(pair_in[(w,) + k].values()) <= now
+                ]
+            quota = routes.quota[w] if i < steps and (j > 0 or got) else never
+            sums_here = sum(o[0] in "XZF" for o in slots[w].get((i, j), ()))
+            if sums_here >= quota:
+                open_ops = [o for o in open_ops if o[0] in "tocv"]
             if open_ops:
                 op = min(open_ops, key=lambda o: precedence(w, o))
                 todo[w].remove(op)
@@ -233,12 +245,7 @@
                 continue
             if i < steps:
                 if j == 0:
-                    got = [
-                        k for k in pairs[w]
-                        if len(pair_in.get((w,) + k, {})) == pieces
-                        and max(pair_in[(w,) + k].values()) <= now
-                    ]
-                    if not got or now < 2.5:
+                    if not got:
                         continue
                     pairs[w].remove(got[0])
                     order[w].append(got[0])
@@ -269,9 +276,9 @@
 
 
 def exchange_kernel(
-    ids_hbm, share_hbm, tok_hbm, gate_hbm, up_hbm, down_hbm, out_ref,
-    ids_ref, share_ref, x_buf, gate_w, up_w, down_w, hid, mixer, sums, quad, over, flow,
-    load_sem, x_s, xp_s, q_s, sum_s, x_r, xp_r, q_r, over_r, flow_r,
+    ids_hbm, share_hbm, tok_hbm, gate_hbm, up_hbm, down_hbm, out_hbm,
+    ids_ref, share_ref, x_buf, gate_w, up_w, down_w, hid, mixer, sums, quad, over, flow, result,
+    load_sem, x_s, xp_s, q_s, sum_s, x_r, xp_r, q_r, over_r, flow_r, out_s,
     *, members, capacity, routes,
 ):
     length, pieces, half = routes.length, routes.pieces, routes.half
@@ -402,6 +409,11 @@
     def answer_copy(zz, xx):
         return send(
             sums.at[zz, xx, 1 - c], quad.at[zz, xx], q_s.at[zz, xx], q_r.at[zz, xx], partner
+        )
+
+    def result_copy(q):
+        return pltpu.make_async_copy(
+            result.at[stretch(q)], out_hbm.at[stretch(q)], out_s.at[q]
         )
 
     def over_copy(zz, xx, q, count=1):
@@ -438,7 +450,8 @@
                 total += flow[lane(d), zz, xx, stretch(q)].astype(jnp.float32)
             total = total.astype(jnp.bfloat16)
             if kind == "F" and col == 0:
-                out_ref[stretch(q), :] = total
+                result[stretch(q), :] = total
+                result_copy(q).start()
                 return
             sums[zz, xx, c, stretch(q)] = total
             if leaves:
@@ -591,6 +604,8 @@
         return carry
 
     lax.fori_loop(0, length, drain, 0)
+    for q in range(routes.parts):
+        result_copy(q).wait()
 
 
 def gathered_plan(tokens, expert_ids, combine, gate_proj, up_proj, down_proj, capacity):
@@ -606,14 +621,13 @@
     dma = pltpu.SemaphoreType.DMA
     vmem = lambda *shape: pltpu.VMEM(shape, jnp.bfloat16)
     anywhere = pl.BlockSpec(memory_space=pl.ANY)
-    inside = pl.BlockSpec(memory_space=pltpu.VMEM)
     return pl.pallas_call(
         functools.partial(
             exchange_kernel, members=members, capacity=capacity, routes=routes
         ),
         out_shape=jax.ShapeDtypeStruct(block, jnp.bfloat16),
         in_specs=[anywhere, anywhere, anywhere, anywhere, anywhere, anywhere],
-        out_specs=inside,
+        out_specs=anywhere,
         scratch_shapes=[
             pltpu.VMEM(expert_ids.shape[::-1], jnp.int32),
             pltpu.VMEM(combine.shape[::-1], jnp.float32),
@@ -621,11 +635,11 @@
             vmem(features, ff), vmem(features, ff), vmem(ff, features),
             vmem(2 * capacity, ff), vmem(2 * capacity, 2 * here),
             vmem(length, 2, 2, *block), vmem(length, 2, *block),
-            vmem(length, *block), vmem(2, length, 2, *block),
+            vmem(length, *block), vmem(2, length, 2, *block), vmem(*block),
             dma((6,)), dma((length, 2, 3)), dma((length, 2)),
             dma((length, 2)), dma((length, 2, 2)),
             dma((length, 2, pieces)), dma((length, 2)), dma((length, 2)),
-            dma((length, parts)), dma((2, length, 2, parts)),
+            dma((length, parts)), dma((2, length, 2, parts)), dma((parts,)),
         ],
         compiler_params=pltpu.CompilerParams(
             collective_id=0, has_side_effects=True, vmem_limit_bytes=60 * 1024 * 1024

time: 66.2 us -> 65.3 us (0.986)
  Pallas kernels: 64.3 us -> 63.3 us
    pallas_call x1, Pallas kernels: 64.3 us -> 63.3 us  [gathered_plan(): pl.pallas_call(functools.partial(exchange_kernel, members=members, capaci...]
where the time goes in v4:
time: 65.3 us; the launch traced here: 65 us
  Pallas kernels  63.3 us (97%)
  local copies, waits for them, and re-layouts  1.75 us (3%)
    pallas_call x1, Pallas kernels, gathered_plan(): pl.pallas_call(functools.partial(exchange_kernel, members=members, capaci...  63.3 us
    unnamed x1, local copies, waits for them, and re-layouts  1.75 us

profile of v4, /device:TPU:0, one launch (start us, length us, event | category | flops | bytes accessed | tf_op | source)
XLA Modules:
  0.0 65.0 jit_solution(5100802470419622834)
XLA Ops:
  0.0 63.3 %shard_map.64 = bf16[1440,128]{1,0:T(8,128)(2,1)} custom-call(s32[4,128]{1,0:T(4,128)} %bitcast.12, f32[4,128]{1,0:T(4,128)} %bitcast.13, bf16[1440,128]{1,0:T(8,128)(2,1)} %bitcast.11, bf16[1440,1440]{1,0:T(8,128)(2,1)} %bitcast.7, bf16[1440,1440]{1,0:T(8,128)(2,1)} %bitcast.8, bf16[1440,1440]{1,0:T(8,128)(2,1)} %bitcast.9), custom_call_target="tpu_custom_call" | custom-call | tf_op jit(solution)/shard_map/pallas_call | solution.py:624
  63.3 1.7 %copy.8 = bf16[128,1440]{0,1:T(8,128)(2,1)} copy(bf16[128,1440]{0,1:T(8,128)(2,1)} %bitcast.10) | data formatting | bytes 737280

commit v5 on v4

--- a/solution.py
+++ b/solution.py
@@ -564,7 +564,7 @@
                 value = jnp.where(here_now, order[w][n][k], value)
         return value
 
-    for load in loads[1:]:
+    for load in loads[1:3]:
         load.wait()
 
     def step_of(i, carry):
@@ -574,6 +574,7 @@
         partner_copy(zz, xx).wait_recv()
         inner(zz, xx)
         run_slot(i, 1)
+        pl.when(i == 0)(loads[3].wait)
         outer(zz, xx)
         answer_copy(zz, xx).start()
         return carry

time: 65.3 us -> 64.8 us (level)
  no operation moved by 1% of the time
where the time goes in v5:
time: 64.8 us; the launch traced here: 64.7 us
  Pallas kernels  62.9 us (97%)
  local copies, waits for them, and re-layouts  1.75 us (3%)
    pallas_call x1, Pallas kernels, gathered_plan(): pl.pallas_call(functools.partial(exchange_kernel, members=members, capaci...  62.9 us
    unnamed x1, local copies, waits for them, and re-layouts  1.75 us

profile of v5, /device:TPU:0, one launch (start us, length us, event | category | flops | bytes accessed | tf_op | source)
XLA Modules:
  0.0 64.7 jit_solution(7441164074001050527)
XLA Ops:
  0.0 62.9 %shard_map.64 = bf16[1440,128]{1,0:T(8,128)(2,1)} custom-call(s32[4,128]{1,0:T(4,128)} %bitcast.12, f32[4,128]{1,0:T(4,128)} %bitcast.13, bf16[1440,128]{1,0:T(8,128)(2,1)} %bitcast.11, bf16[1440,1440]{1,0:T(8,128)(2,1)} %bitcast.7, bf16[1440,1440]{1,0:T(8,128)(2,1)} %bitcast.8, bf16[1440,1440]{1,0:T(8,128)(2,1)} %bitcast.9), custom_call_target="tpu_custom_call" | custom-call | tf_op jit(solution)/shard_map/pallas_call | solution.py:625
  62.9 1.7 %copy.8 = bf16[128,1440]{0,1:T(8,128)(2,1)} copy(bf16[128,1440]{0,1:T(8,128)(2,1)} %bitcast.10) | data formatting | bytes 737280
